TPU v7x, 32 devices: a whole 2x2x4 slice. The times are simulated.
32 devices in a mesh: chan: 4 (over z), pulse: 4 (over x, core), range: 2 (over y).
Axes of the slice: x: 2, y: 2, z: 4, core: 2. Of those that a mesh axis runs over, the one named last changes fastest.
Arguments:
- signal: bfloat16 [2, 64, 32, 8192], P(None, 'chan', 'pulse', 'range'), may hold values from -6 to 6
- steering: bfloat16 [2, 32, 64], replicated, may hold values from -0.5 to 0.5
- spectrum: float32 [2, 8192], replicated, may hold values from -6 to 6
Outputs:
- detection: float32 [32, 32, 8192], P('chan', 'pulse', 'range')
All inputs are finite; a program needn't handle non-finite values.
Results may differ from a plain program's by a relative error of at most 0.0087.
Values may be sent and summed in bfloat16 or wider, within the bound.
No kernel may reach another device: no remote copies, remote signals or barrier semaphores. Data moves between devices by JAX's collectives and lax.ppermute only.
A program may use at most 64 MiB of HBM per device.

v0:
```python
import math

import jax
import jax.numpy as jnp
from jax import lax
from jax.sharding import PartitionSpec as P

GUARD = 4
TRAIN = 16


PRECISE = lax.Precision.HIGHEST
NOISE_FLOOR = 0.25


def padded_2(x, sides, width):
    for axis, dim in sides:
        peers, length = (lax.axis_size(axis), x.shape[dim])
        up = [(i, (i + 1) % peers) for i in range(peers - 1)]
        down = [(j, i) for i, j in up]
        last = lax.slice_in_dim(x, length - width, length, axis=dim)
        initial = lax.slice_in_dim(x, 0, width, axis=dim)
        before = lax.ppermute(last, axis, up)
        after = lax.ppermute(initial, axis, down)
        x = jnp.concatenate([before, x, after], axis=dim)
    return x


def doppler_tables(pulse_count):
    row_ids = lax.broadcasted_iota(jnp.int32, (pulse_count, pulse_count), 0)
    col_ids = lax.broadcasted_iota(jnp.int32, (pulse_count, pulse_count), 1)
    phase_angle = (row_ids * col_ids % pulse_count).astype(jnp.float32) * (
        2.0 * math.pi / pulse_count
    )
    norm_scale = 1.0 / math.sqrt(pulse_count)
    table_real = (jnp.cos(phase_angle) * norm_scale).astype(jnp.bfloat16)
    table_imag = (-jnp.sin(phase_angle) * norm_scale).astype(jnp.bfloat16)
    return (table_real, table_imag)


def phase_table(row_count, col_count, period_len, direction):
    row_ids = lax.broadcasted_iota(jnp.int32, (row_count, col_count), 0)
    col_ids = lax.broadcasted_iota(jnp.int32, (row_count, col_count), 1)
    phase_angle = (row_ids * col_ids % period_len).astype(jnp.float32) * (
        2.0 * math.pi / period_len
    )
    return (jnp.cos(phase_angle), direction * jnp.sin(phase_angle))


def rotate_by(field_pair, table_pair):
    return (
        field_pair[0] * table_pair[0] - field_pair[1] * table_pair[1],
        field_pair[0] * table_pair[1] + field_pair[1] * table_pair[0],
    )


def mix_blocks(table_pair, field_pair):

    def contract(table_part, field_part):
        return jnp.einsum("km,bpmn->bpkn", table_part, field_part, precision=PRECISE)

    return (
        contract(table_pair[0], field_pair[0]) - contract(table_pair[1], field_pair[1]),
        contract(table_pair[0], field_pair[1]) + contract(table_pair[1], field_pair[0]),
    )


def mix_lanes(field_pair, table_pair):

    def contract(field_part, table_part):
        return jnp.einsum("bpkm,mn->bpkn", field_part, table_part, precision=PRECISE)

    return (
        contract(field_pair[0], table_pair[0]) - contract(field_pair[1], table_pair[1]),
        contract(field_pair[0], table_pair[1]) + contract(field_pair[1], table_pair[0]),
    )


def local_transform(field_pair, direction):
    size_all = field_pair[0].shape[-1]
    blocks = size_all // 128
    leading = field_pair[0].shape[:-1]
    shaped = tuple((member.reshape(leading + (blocks, 128)) for member in field_pair))
    outer_table = phase_table(blocks, blocks, blocks, direction)
    twiddle = phase_table(blocks, 128, size_all, direction)
    inner_table = phase_table(128, 128, 128, direction)
    if direction < 0:
        shaped = mix_blocks(outer_table, shaped)
        shaped = rotate_by(shaped, twiddle)
        shaped = mix_lanes(shaped, inner_table)
    else:
        shaped = mix_lanes(shaped, inner_table)
        shaped = rotate_by(shaped, twiddle)
        shaped = mix_blocks(outer_table, shaped)
    return tuple((member.reshape(leading + (size_all,)) for member in shaped))


def stack_weights(w_real, w_imag):
    return jnp.concatenate(
        [jnp.concatenate([w_real, -w_imag], 1), jnp.concatenate([w_imag, w_real], 1)], 0
    )


def shards(signal, steering, spectrum):
    beam_count = steering.shape[1]
    chan_count = steering.shape[2]
    pulse_local = signal.shape[2]
    gate_count = signal.shape[3]
    stacked = stack_weights(steering[0], steering[1])
    samples = lax.all_to_all(signal, "chan", split_axis=2, concat_axis=1, tiled=True)
    pulses_here = samples.shape[2]
    gates_here = samples.shape[3]
    flat_samples = samples.reshape(2 * chan_count, pulses_here * gates_here)
    formed = jnp.dot(stacked, flat_samples, preferred_element_type=jnp.float32)
    formed = formed.astype(jnp.bfloat16).reshape(2, beam_count, pulses_here, gates_here)
    beam_data = lax.all_to_all(formed, "chan", split_axis=1, concat_axis=2, tiled=True)
    beam_local = beam_data.shape[1]
    range_count = lax.axis_size("range")
    range_index = lax.axis_index("range")
    full_length = gate_count * range_count
    inverse_scale = 1.0 / full_length
    shard_piece = lax.all_gather(beam_data, "range", axis=3, tiled=True)
    shard_count = shard_piece.shape[3] // gate_count
    members = shard_piece.astype(jnp.float32).reshape(
        2, beam_local, pulse_local, shard_count, gate_count
    )
    source = jnp.arange(shard_count, dtype=jnp.int32)
    phase_angle = (source * range_index % range_count).astype(jnp.float32) * (
        2.0 * math.pi / range_count
    )
    cos_part = jnp.cos(phase_angle)[:, None]
    sin_part = -jnp.sin(phase_angle)[:, None]
    sum_real = jnp.sum(members[0] * cos_part - members[1] * sin_part, axis=2)
    sum_imag = jnp.sum(members[0] * sin_part + members[1] * cos_part, axis=2)
    folded = (sum_real, sum_imag)
    gate_ids = lax.broadcasted_iota(jnp.int32, (gate_count,), 0)
    global_angle = (gate_ids * range_index % full_length).astype(jnp.float32) * (
        2.0 * math.pi / full_length
    )
    folded = rotate_by(folded, (jnp.cos(global_angle), -jnp.sin(global_angle)))
    spectrum_local = local_transform(folded, -1.0)
    response = spectrum.reshape(2, gate_count, range_count)
    response = lax.dynamic_index_in_dim(response, range_index, axis=2, keepdims=False)
    response = jnp.transpose(response.reshape(2, 128, gate_count // 128), (0, 2, 1)).reshape(
        2, gate_count
    )
    filtered = rotate_by(spectrum_local, (response[0], response[1]))
    restored = local_transform(filtered, 1.0)
    restored = rotate_by(restored, (jnp.cos(global_angle), jnp.sin(global_angle)))
    shard_piece = (
        lax.all_gather(restored[0], "range", axis=2, tiled=True),
        lax.all_gather(restored[1], "range", axis=2, tiled=True),
    )
    shard_count = shard_piece[0].shape[2] // gate_count
    rows_real = shard_piece[0].reshape(beam_local, pulse_local, shard_count, gate_count)
    rows_imag = shard_piece[1].reshape(beam_local, pulse_local, shard_count, gate_count)
    source = jnp.arange(shard_count, dtype=jnp.int32)
    phase_angle = (source * range_index % range_count).astype(jnp.float32) * (
        2.0 * math.pi / range_count
    )
    cos_part = jnp.cos(phase_angle)[:, None]
    sin_part = jnp.sin(phase_angle)[:, None]
    sum_real = jnp.sum(rows_real * cos_part - rows_imag * sin_part, axis=2)
    sum_imag = jnp.sum(rows_real * sin_part + rows_imag * cos_part, axis=2)
    compressed = jnp.stack([sum_real * inverse_scale, sum_imag * inverse_scale]).astype(
        jnp.bfloat16
    )
    pulse_total = pulse_local * lax.axis_size("pulse")
    dop_real, dop_imag = doppler_tables(pulse_total)
    columns = lax.all_to_all(compressed, "pulse", split_axis=3, concat_axis=2, tiled=True)

    def product(table_part, values):
        return jnp.einsum("fp,bpr->bfr", table_part, values, preferred_element_type=jnp.float32)

    mixed_real = product(dop_real, columns[0]) - product(dop_imag, columns[1])
    mixed_imag = product(dop_real, columns[1]) + product(dop_imag, columns[0])
    power_part = lax.all_to_all(
        mixed_real * mixed_real + mixed_imag * mixed_imag,
        "pulse",
        split_axis=1,
        concat_axis=2,
        tiled=True,
    )
    halo_width = GUARD + TRAIN
    padded = padded_2(power_part, (("range", 2),), halo_width)
    window_sum = jnp.zeros_like(power_part)
    for offset in range(1, TRAIN + 1):
        left_start = halo_width - GUARD - offset
        right_start = halo_width + GUARD + offset
        window_sum = (
            window_sum
            + padded[:, :, left_start : left_start + gate_count]
            + padded[:, :, right_start : right_start + gate_count]
        )
    noise_level = window_sum / (2.0 * TRAIN)
    return power_part / (noise_level + NOISE_FLOOR)


def solution(mesh):
    in_specs = (P(None, "chan", "pulse", "range"), P(), P())
    out_specs = P("chan", "pulse", "range")
    return jax.shard_map(shards, mesh=mesh, in_specs=in_specs, out_specs=out_specs, check_vma=False)
```

profile of v0, /device:TPU:0, one launch (start us, length us, event | category | flops | bytes accessed | tf_op | source)
XLA Modules:
  0.0 388.4 jit_solution(4963313028370823325)
XLA Ops:
  6.5 4.1 %copy.81 = bf16[2,16,8,4096]{3,1,0,2:T(8,128)(2,1)} copy(bf16[2,16,8,4096]{3,2,1,0:T(8,128)(2,1)} %param.3) | data formatting | bytes 4194304 | tf_op args[0]
  10.6 6.5 %all-to-all-start = ((bf16[2,16,8,4096]{3,1,0,2:T(8,128)(2,1)}), bf16[2,16,8,4096]{3,1,0,2:T(8,128)(2,1)S(1)}, u32[]{:S(2)}, u32[]{:S(2)}) async-start(bf16[2,16,8,4096]{3,1,0,2:T(8,128)(2,1)} %copy.81), calls=%async_computation | async-start | bytes 4194304 | tf_op jit(solution)/shard_map/all_to_all | solution.py:110
  17.1 48.2 %all-to-all-done = bf16[2,16,8,4096]{3,1,0,2:T(8,128)(2,1)S(1)} async-done(((bf16[2,16,8,4096]{3,1,0,2:T(8,128)(2,1)}), bf16[2,16,8,4096]{3,1,0,2:T(8,128)(2,1)S(1)}, u32[]{:S(2)}, u32[]{:S(2)}) %all-to-all-start) | async-done | bytes 2097184 | tf_op jit(solution)/shard_map/all_to_all | solution.py:110
  71.0 27.7 %all_to_all.66 = bf16[2,32,2,4096]{3,2,0,1:T(2,128)(2,1)S(1)} all-to-all(bf16[2,32,2,4096]{3,2,0,1:T(2,128)(2,1)S(1)} %copy.83), channel_id=1, replica_groups=mesh['chan'=4,'pulse'=4,'range'=2] {'chan'}, dimensions={1} | all-to-all | bytes 2097152 | tf_op jit(solution)/shard_map/all_to_all | solution.py:116
  100.6 6.4 %reshape.188 = f32[2,4096,2]{2,1,0:T(8,128)} reshape(f32[2,8192]{1,0:T(2,128)S(1)} %copy-done.1) | data formatting | bytes 131072 | tf_op jit(solution)/shard_map/reshape | solution.py:142
  107.0 4.7 %dynamic-slice_reduce_fusion = f32[2,4096]{1,0:T(2,128)S(1)} fusion(f32[2,4096,2]{2,1,0:T(8,128)} %reshape.188, s32[]{:T(128)S(6)} %select_n.134), kind=kLoop, calls=%fused_computation.31 | loop fusion | bytes 65540 | tf_op jit(solution)/shard_map/jit(dynamic_index_in_dim)/dynamic_slice | solution.py:143
  112.5 20.2 %all-gather.4.cloned.1.call-done = bf16[2,8,8,8192]{3,1,2,0:T(8,128)(2,1)} async-done(((bf16[2,8,8,4096]{3,1,2,0:T(8,128)(2,1)}), bf16[2,8,8,8192]{3,1,2,0:T(8,128)(2,1)}) %all-gather.4.cloned.1.call-update) | async-done | bytes 2097168 | tf_op jit(solution)/shard_map/all_gather | solution.py:122
  132.7 3.9 %fusion.271 = (f32[1,8,8,8192]{3,1,2,0:T(8,128)}, f32[1,8,8,8192]{3,1,2,0:T(8,128)}) fusion(bf16[2,8,8,8192]{3,1,2,0:T(8,128)(2,1)} %all-gather.4.cloned.1.call-done), kind=kLoop, calls=%fused_computation.365 | loop fusion | bytes 8388608 | tf_op jit(solution)/shard_map/slice | solution.py:133
  136.6 3.0 reshape.202
  139.7 4.4 %reshape.203 = f32[8,8,2,4096]{3,2,0,1:T(2,128)} reshape(f32[1,8,8,8192]{3,1,2,0:T(8,128)} %get-tuple-element.12) | data formatting | bytes 4194304 | tf_op jit(solution)/shard_map/squeeze | solution.py:133
  144.1 5.8 %subtract_reduce_fusion.1 = (f32[8,8,4096]{2,1,0:T(8,128)S(1)}, f32[8,8,4096]{2,1,0:T(8,128)S(1)}) fusion(f32[8,8,2,4096]{3,2,0,1:T(2,128)} %reshape.203, f32[8,8,2,4096]{3,2,0,1:T(2,128)S(1)} %reshape.202, f32[2]{0:T(128)S(1)} %get-tuple-element.24, f32[2]{0:T(128)S(1)} %get-tuple-element.23), kind=kLoop, calls=%fused_computation.35 | loop fusion | flops 3670016 | bytes 6291472 | tf_op jit(solution)/shard_map/reduce_sum | solution.py:133
  172.0 2.4 reshape.191
  180.4 32.5 %all-gather.6.cloned.1.call-done = f32[8,8,8192]{2,1,0:T(8,128)} async-done(((f32[8,8,4096]{2,1,0:T(8,128)}), f32[8,8,8192]{2,1,0:T(8,128)}) %all-gather.6.cloned.1.call-update) | async-done | bytes 2097168 | tf_op jit(solution)/shard_map/all_gather | solution.py:151
  212.9 34.7 %all-gather.8.cloned.1.call-done = f32[8,8,8192]{2,1,0:T(8,128)} async-done(((f32[8,8,4096]{2,1,0:T(8,128)}), f32[8,8,8192]{2,1,0:T(8,128)}) %all-gather.8.cloned.1.call-update) | async-done | bytes 2097168 | tf_op jit(solution)/shard_map/all_gather | solution.py:152
  247.6 3.2 subtract_reduce_fusion
  252.1 14.0 %copy.106 = bf16[2,8,8,4096]{2,1,0,3:T(8,128)(2,1)} copy(bf16[2,8,8,4096]{3,1,2,0:T(8,128)(2,1)S(1)} %pad_maximum_fusion.2) | data formatting | bytes 2097152 | tf_op jit(solution)/shard_map/stack | solution.py:165
  266.1 20.5 %reshape.205 = bf16[4,2,65536]{2,1,0:T(2,128)(2,1)S(1)} reshape(bf16[4096,2,8,8]{3,2,1,0:T(8,128)(2,1)} %bitcast.133) | data formatting | bytes 2097152
  286.6 17.2 %all_to_all.67 = bf16[4,2,65536]{2,1,0:T(2,128)(2,1)S(1)} all-to-all(bf16[4,2,65536]{2,1,0:T(2,128)(2,1)S(1)} %reshape.205), channel_id=1, replica_groups=mesh['chan'=4,'pulse'=4,'range'=2] {'pulse'}, dimensions={0} | all-to-all | bytes 2097152 | tf_op jit(solution)/shard_map/all_to_all | solution.py:170
  303.8 21.7 %reshape.206 = bf16[4096,2,8,8]{3,2,1,0:T(8,128)(2,1)} reshape(bf16[4,2,65536]{2,1,0:T(2,128)(2,1)S(1)} %all_to_all.67) | data formatting | bytes 2097152
  325.5 16.0 %copy.107 = bf16[2,8,8,4,1024]{4,2,3,1,0:T(8,128)(2,1)S(1)} copy(bf16[2,8,8,4,1024]{2,1,0,4,3:T(8,128)(2,1)} %bitcast.134) | data formatting | bytes 2097152 | tf_op jit(solution)/shard_map/all_to_all | solution.py:170
  343.6 16.9 %all_to_all.68 = f32[8,32,1024]{2,0,1:T(8,128)S(1)} all-to-all(f32[8,32,1024]{2,0,1:T(8,128)S(1)} %copy.108), channel_id=1, replica_groups=mesh['chan'=4,'pulse'=4,'range'=2] {'pulse'}, dimensions={1} | all-to-all | bytes 2097152 | tf_op jit(solution)/shard_map/all_to_all | solution.py:177
  361.2 2.4 collective-permute-start
  365.2 4.2 %collective-permute-done.1 = f32[8,8,20]{2,1,0:T(8,128)S(1)} collective-permute-done((f32[8,8,20]{2,1,0:T(8,128)S(1)}, f32[8,8,20]{2,1,0:T(8,128)S(1)}, u32[]{:S(2)}, u32[]{:S(2)}) %collective-permute-start.1) | collective-permute-done | bytes 5152 | tf_op jit(solution)/shard_map/ppermute | solution.py:24
  369.4 12.0 %fusion.14 = f32[8,8,4096]{2,1,0:T(8,128)} fusion(f32[8,8,4096]{2,1,0:T(8,128)S(1)} %bitcast.151, f32[8,8,20]{2,1,0:T(8,128)S(1)} %collective-permute-done.1, f32[8,8,20]{2,1,0:T(8,128)S(1)} %collective-permute-done), kind=kLoop, calls=%fused_computation.60 | loop fusion | flops 17301504 | bytes 2107392 | tf_op jit(solution)/shard_map/div | solution.py:196
  (63 shorter events, 42.0 us)
Async XLA Ops:
  10.6 6.5 %copy-start.2 = (bf16[2,32,64]{2,1,0:T(8,128)(2,1)S(1)}, bf16[2,32,64]{2,1,0:T(8,128)(2,1)}, u32[]{:S(2)}) copy-start(bf16[2,32,64]{2,1,0:T(8,128)(2,1)} %param.4) | copy-start | bytes 24580
  10.6 54.7 %all-to-all-start = ((bf16[2,16,8,4096]{3,1,0,2:T(8,128)(2,1)}), bf16[2,16,8,4096]{3,1,0,2:T(8,128)(2,1)S(1)}, u32[]{:S(2)}, u32[]{:S(2)}) async-start(bf16[2,16,8,4096]{3,1,0,2:T(8,128)(2,1)} %copy.81), calls=%async_computation | async-start | bytes 4194304 | tf_op jit(solution)/shard_map/all_to_all | solution.py:110
  17.1 115.6 %all-gather.4.cloned.1.call-start = ((), (), s32[]{:S(2)}) async-start(), calls=%async_computation.4 | async-start | bytes 3145728 | tf_op jit(solution)/shard_map/all_gather | solution.py:122
  99.3 1.3 copy-start.1
  100.4 112.5 %all-gather.6.cloned.1.call-start = ((), (), s32[]{:S(2)}) async-start(), calls=%async_computation.5 | async-start | bytes 3145728 | tf_op jit(solution)/shard_map/all_gather | solution.py:151
  176.5 1.5 copy-start
  179.7 67.9 %all-gather.8.cloned.1.call-start = ((), (), s32[]{:S(2)}) async-start(), calls=%async_computation.6 | async-start | bytes 3145728 | tf_op jit(solution)/shard_map/all_gather | solution.py:152
  361.2 4.0 %collective-permute-start = (f32[8,8,20]{2,1,0:T(8,128)S(1)}, f32[8,8,20]{2,1,0:T(8,128)S(1)}, u32[]{:S(2)}, u32[]{:S(2)}) collective-permute-start(f32[8,8,20]{2,1,0:T(8,128)S(1)} %get-tuple-element.13), channel_id=1, source_target_pairs={{0,1},{2,3},{4,5},{6,7},{8,9},{10,11},{12,13},{14,15},{16,17},{18,... | collective-permute-start | bytes 15368 | tf_op jit(solution)/shard_map/ppermute | solution.py:23
  363.6 5.8 %collective-permute-start.1 = (f32[8,8,20]{2,1,0:T(8,128)S(1)}, f32[8,8,20]{2,1,0:T(8,128)S(1)}, u32[]{:S(2)}, u32[]{:S(2)}) collective-permute-start(f32[8,8,20]{2,1,0:T(8,128)S(1)} %get-tuple-element.14), channel_id=1, source_target_pairs={{1,0},{3,2},{5,4},{7,6},{9,8},{11,10},{13,12},{15,14},{17,16},{19,... | collective-permute-start | bytes 15368 | tf_op jit(solution)/shard_map/ppermute | solution.py:24
Sparse Core Ops, SparseCore 0:
  100.5 32.1 all-gather.3
  179.8 33.0 all-gather.5
  214.5 33.0 all-gather.7
where the time goes:
time: 395 us; the launch traced here: 388 us
  waiting for transfers between devices  141 us (36%)
  local copies, waits for them, and re-layouts  112 us (28%)
  blocking collectives  61.8 us (16%)
  matrix products  24.9 us (6%)
  other arithmetic  24.3 us (6%)
  between operations  13.9 us (4%)
  starting transfers between devices  10.5 us (3%)
    unnamed x12, local copies, waits for them, and re-layouts  48.9 us
    all_to_all x1, waiting for transfers between devices, shards(): lax.all_to_all(signal, 'chan', split_axis=2, concat_axis=1, tiled=True)  48.2 us
    all_gather x1, waiting for transfers between devices, shards(): lax.all_gather(restored[1], 'range', axis=2, tiled=True)  34.7 us
    all_gather x1, waiting for transfers between devices, shards(): lax.all_gather(restored[0], 'range', axis=2, tiled=True)  32.5 us
    all_to_all x1, blocking collectives, shards(): lax.all_to_all(formed, 'chan', split_axis=1, concat_axis=2, tiled=True)  27.7 us
    all_gather x1, waiting for transfers between devices, shards(): shard_piece = lax.all_gather(beam_data, 'range', axis=3, tiled=True)  20.2 us
    all_to_all x1, blocking collectives, shards(): lax.all_to_all(compressed, 'pulse', split_axis=3, concat_axis=2, tiled=True)  17.2 us
    all_to_all x1, blocking collectives, shards(): lax.all_to_all(mixed_real * mixed_real + mixed_imag * mixed_imag, 'pulse'...  16.9 us
  transfers between devices with their start and end apart: 6, of which 6 were waited for; matrix products, arithmetic and copies ran while one was open for 3% of the time, Pallas kernels for 0%

commit v1 on v0

--- a/solution.py
+++ b/solution.py
@@ -1,16 +1,202 @@
+import functools
 import math
 
 import jax
 import jax.numpy as jnp
+import numpy as np
 from jax import lax
+from jax.experimental import pallas as pl
+from jax.experimental.pallas import tpu as pltpu
 from jax.sharding import PartitionSpec as P
 
 GUARD = 4
 TRAIN = 16
+NOISE_FLOOR = 0.25
+LANES = 128
+
+
+def dft_pair(n):
+    ids = np.arange(n)
+    angle = 2.0 * np.pi * (np.outer(ids, ids) % n) / n
+    return np.cos(angle), np.sin(angle)
+
+
+def range_tables(length):
+    rows = length // LANES
+    cos1, sin1 = dft_pair(rows)
+    cos2, sin2 = dft_pair(LANES)
+    left_fwd = np.block([[cos1, sin1], [-sin1, cos1]])
+    left_inv = np.block([[cos1, -sin1], [sin1, cos1]])
+    right_fwd = np.block([[cos2, -sin2], [sin2, cos2]])
+    right_inv = np.block([[cos2, sin2], [-sin2, cos2]])
+    angle = 2.0 * np.pi * (np.outer(np.arange(rows), np.arange(LANES)) % length) / length
+    twiddle = np.stack([np.cos(angle), -np.sin(angle)])
+    mats = [jnp.asarray(m, jnp.bfloat16) for m in (left_fwd, left_inv, right_fwd, right_inv)]
+    return mats + [jnp.asarray(twiddle, jnp.float32)]
+
+
+def doppler_matrix(pulses):
+    ids = np.arange(pulses)
+    angle = 2.0 * np.pi * (np.outer(ids, ids) % pulses) / pulses
+    scale = 1.0 / math.sqrt(pulses)
+    real, imag = np.cos(angle) * scale, -np.sin(angle) * scale
+    return jnp.asarray(np.block([[real, -imag], [imag, real]]), jnp.bfloat16)
+
+
+def filter_kernel(
+    beams, rows, x_ref, w_ref, lf_ref, li_ref, rf_ref, ri_ref, tw_ref, h_ref, out_ref, s_ref, a_ref
+):
+    blocks = x_ref.shape[1]
+    gates = x_ref.shape[4]
+    depth = w_ref.shape[1]
+    per_block = gates // LANES
+    wide = 8
+    for block in range(blocks):
+        for step in range(per_block // wide):
+            lanes = pl.ds(step * wide * LANES, wide * LANES)
+            x = x_ref[:, block, :, :, lanes].reshape(depth, wide * LANES)
+            y = jnp.dot(w_ref[...], x, preferred_element_type=jnp.float32)
+            for i in range(wide):
+                n1 = block * per_block + step * wide + i
+                s_ref[pl.ds(n1, 2 * beams, stride=rows), :] = y[:, i * LANES : (i + 1) * LANES]
+    group = 4
+    scale = 1.0 / (rows * LANES)
+    tw_re, tw_im = tw_ref[0], tw_ref[1]
+    h_re, h_im = h_ref[0], h_ref[1]
+
+    def spun(z, c_re, c_im):
+        re, im = z[:, :LANES], z[:, LANES:]
+        return jnp.concatenate([re * c_re - im * c_im, re * c_im + im * c_re], 1)
+
+    def body(g, carry):
+        for i in range(group):
+            b = g * group + i
+            re = s_ref[pl.ds(pl.multiple_of(b * rows, rows), rows), :]
+            im = s_ref[pl.ds(pl.multiple_of((b + beams) * rows, rows), rows), :]
+            z = jnp.concatenate([re, im], 0).astype(jnp.bfloat16)
+            a = jnp.dot(lf_ref[...], z, preferred_element_type=jnp.float32)
+            z = spun(jnp.concatenate([a[:rows], a[rows:]], 1), tw_re, tw_im)
+            a_ref[pl.ds(i * rows, rows), :] = z.astype(jnp.bfloat16)
+        c = jnp.dot(a_ref[...], rf_ref[...], preferred_element_type=jnp.float32)
+        d = jnp.concatenate(
+            [spun(c[i * rows : (i + 1) * rows], h_re, h_im) for i in range(group)], 0
+        ).astype(jnp.bfloat16)
+        e = jnp.dot(d, ri_ref[...], preferred_element_type=jnp.float32)
+        for i in range(group):
+            b = g * group + i
+            z = spun(e[i * rows : (i + 1) * rows], tw_re * scale, -tw_im * scale)
+            z = jnp.concatenate([z[:, :LANES], z[:, LANES:]], 0).astype(jnp.bfloat16)
+            o = jnp.dot(li_ref[...], z, preferred_element_type=jnp.float32)
+            out_ref[b] = o.astype(jnp.bfloat16)
+        return carry
+
+    lax.fori_loop(0, beams // group, body, 0)
+
+
+def detect_kernel(pulses, rows, z_ref, d_ref, out_ref, s_ref, p_ref):
+    parts, halves, bins, gates = out_ref.shape
+    length = rows * LANES
+    for p in range(pulses):
+        s_ref[pl.ds(p * 2 * rows, 2 * rows), :] = z_ref[p].astype(jnp.float32)
+    p_ref[:, pl.ds(0, LANES)] = jnp.zeros((pulses, LANES), jnp.float32)
+    p_ref[:, pl.ds(LANES + length, LANES)] = jnp.zeros((pulses, LANES), jnp.float32)
+    wide = 8
+
+    def body(step, carry):
+        cols = []
+        for i in range(wide):
+            j = step * wide + i
+            re = s_ref[pl.ds(j, pulses, stride=2 * rows), :]
+            im = s_ref[pl.ds(j + rows, pulses, stride=2 * rows), :]
+            cols.append(jnp.concatenate([re, im], 0).astype(jnp.bfloat16))
+        m = jnp.dot(d_ref[...], jnp.concatenate(cols, 1), preferred_element_type=jnp.float32)
+        re, im = m[:pulses], m[pulses:]
+        at = pl.multiple_of(LANES + step * wide * LANES, LANES)
+        p_ref[:, pl.ds(at, wide * LANES)] = re * re + im * im
+        return carry
+
+    lax.fori_loop(0, rows // wide, body, 0)
+    span = length + 2 * LANES
+    for q in range(parts):
+        power = p_ref[pl.ds(q * bins, bins), :]
+        total, width = power, 1
+        while width < TRAIN:
+            total = total + pltpu.roll(total, span - width, 1)
+            width *= 2
+        noise = pltpu.roll(total, GUARD + TRAIN, 1) + pltpu.roll(total, span - GUARD - 1, 1)
+        found = power / (noise * (1.0 / (2 * TRAIN)) + NOISE_FLOOR)
+        for s in range(halves):
+            out_ref[q, s] = found[:, LANES + s * gates : LANES + (s + 1) * gates].astype(
+                jnp.bfloat16
+            )
+
+
+def stack_weights(w_real, w_imag):
+    return jnp.concatenate(
+        [jnp.concatenate([w_real, -w_imag], 1), jnp.concatenate([w_imag, w_real], 1)], 0
+    )
+
+
+def vmem_call(kernel, out_shape, scratch, flops, *args):
+    return pl.pallas_call(
+        kernel,
+        out_shape=out_shape,
+        in_specs=[pl.BlockSpec(memory_space=pltpu.VMEM)] * len(args),
+        out_specs=pl.BlockSpec(memory_space=pltpu.VMEM),
+        scratch_shapes=scratch,
+        cost_estimate=pl.CostEstimate(flops=flops, bytes_accessed=0, transcendentals=0),
+        compiler_params=pltpu.CompilerParams(vmem_limit_bytes=48 * 1024 * 1024),
+    )(*args)
+
+
+def lines(signal, steering, spectrum):
+    chans, pulses_n, halves = (lax.axis_size(a) for a in ("chan", "pulse", "range"))
+    beams, channels = steering.shape[1:]
+    pulse_local, gates = signal.shape[2:]
+    pulses, length = pulse_local * pulses_n, gates * halves
+    rows = length // LANES
+    chan_local = channels // chans
+    parts = pulses_n * halves
+    everyone = ("pulse", "chan", "range")
+
+    moved = jnp.transpose(signal, (2, 0, 1, 3))
+    moved = lax.all_to_all(moved, ("chan", "range"), 0, 0, tiled=True)
+    moved = moved.reshape(chans, halves, 2, chan_local, gates)
+
+    weights = steering.reshape(2, chans, pulses_n, halves, channels)
+    weights = jnp.transpose(weights, (0, 2, 1, 3, 4)).reshape(2, beams, channels)
+    weights = stack_weights(weights[0], weights[1]).reshape(2 * beams, 2, chans, chan_local)
+    weights = jnp.transpose(weights, (0, 2, 1, 3)).reshape(2 * beams, 2 * channels)
+    response = jnp.transpose(spectrum.reshape(2, LANES, rows), (0, 2, 1))
+    lf, li, rf, ri, twiddle = range_tables(length)
+    compressed = vmem_call(
+        functools.partial(filter_kernel, beams, rows),
+        jax.ShapeDtypeStruct((beams, 2 * rows, LANES), jnp.bfloat16),
+        [
+            pltpu.VMEM((2 * beams * rows, LANES), jnp.float32),
+            pltpu.VMEM((4 * rows, 2 * LANES), jnp.bfloat16),
+        ],
+        2_000_000_000,
+        moved, weights, lf, li, rf, ri, twiddle, response,
+    )
+    columns = lax.all_to_all(compressed, everyone, 0, 0, tiled=True)
+    bins = pulses // pulses_n
+    found = vmem_call(
+        functools.partial(detect_kernel, pulses, rows),
+        jax.ShapeDtypeStruct((pulses_n, halves, bins, gates), jnp.bfloat16),
+        [
+            pltpu.VMEM((pulses * 2 * rows, LANES), jnp.float32),
+            pltpu.VMEM((pulses, length + 2 * LANES), jnp.float32),
+        ],
+        2_000_000_000,
+        columns, doppler_matrix(pulses),
+    )
+    found = found.reshape(parts, bins, gates)
+    found = lax.all_to_all(found, ("pulse", "range"), 0, 0, tiled=True)
+    return found.astype(jnp.float32)
 
 
 PRECISE = lax.Precision.HIGHEST
-NOISE_FLOOR = 0.25
 
 
 def padded_2(x, sides, width):
@@ -95,13 +281,7 @@
     return tuple((member.reshape(leading + (size_all,)) for member in shaped))
 
 
-def stack_weights(w_real, w_imag):
-    return jnp.concatenate(
-        [jnp.concatenate([w_real, -w_imag], 1), jnp.concatenate([w_imag, w_real], 1)], 0
-    )
-
-
-def shards(signal, steering, spectrum):
+def blocks(signal, steering, spectrum):
     beam_count = steering.shape[1]
     chan_count = steering.shape[2]
     pulse_local = signal.shape[2]
@@ -199,4 +379,14 @@
 def solution(mesh):
     in_specs = (P(None, "chan", "pulse", "range"), P(), P())
     out_specs = P("chan", "pulse", "range")
+
+    def shards(signal, steering, spectrum):
+        sizes = {a: lax.axis_size(a) for a in mesh.axis_names}
+        beam_local = steering.shape[1] // sizes["chan"]
+        if beam_local == sizes["pulse"] * sizes["range"] and signal.shape[2] == (
+            sizes["chan"] * sizes["range"]
+        ):
+            return lines(signal, steering, spectrum)
+        return blocks(signal, steering, spectrum)
+
     return jax.shard_map(shards, mesh=mesh, in_specs=in_specs, out_specs=out_specs, check_vma=False)

time: 395 us -> 114 us (0.29); the launches traced: 388 us -> 114 us
  local copies, waits for them, and re-layouts: 112 us -> 4.58 us
  waiting for transfers between devices: 141 us -> 47.6 us
  matrix products: 24.9 us -> 0 us
  other arithmetic: 24.3 us -> 1.13 us
  blocking collectives: 61.8 us -> 42.2 us
  between operations: 13.9 us -> 0.14 us
  Pallas kernels: 0 us -> 10.5 us
    all_gather x3 -> x0, waiting for transfers between devices: 87.4 us -> none  [the longest x1 34.7 us: shards(): lax.all_gather(restored[1], 'range', axis=2, tiled=True)]
    unnamed x12 -> x17, local copies, waits for them, and re-layouts: 48.9 us -> 4.12 us
    dot_general x21 -> x0, matrix products: 24.9 us -> none  [the longest x8 12.9 us: contract(): jnp.einsum('km,bpmn->bpkn', table_part, field_part, precision=PRECISE)]
    all_to_all x5 -> x0, local copies, waits for them, and re-layouts: 20.4 us -> none  [the longest x1 16 us: shards(): lax.all_to_all(compressed, 'pulse', split_axis=3, concat_axis=2, tiled=True)]
    all_to_all x3 -> x2, blocking collectives: 61.8 us -> 42.2 us  [the longest x1 30.9 us: lines(): columns = lax.all_to_all(compressed, everyone, 0, 0, tiled=True)]
    another operation x1 -> x0, local copies, waits for them, and re-layouts: 14 us -> none  [shards(): jnp.stack([sum_real * inverse_scale, sum_imag * inverse_scale])]
    div x1 -> x0, other arithmetic: 12 us -> none  [shards(): return power_part / (noise_level + NOISE_FLOOR)]
    reshape x6 -> x4, local copies, waits for them, and re-layouts: 12.1 us -> 0.33 us  [the longest x2 0.22 us: lines(): response = jnp.transpose(spectrum.reshape(2, LANES, rows), (0, 2, 1))]
  transfers between devices with their start and end apart: 6 -> 1, of which waited for: 6 -> 1; matrix products, arithmetic and copies ran while one was open for 3% -> 0% of each run, Pallas kernels for 0% -> 0%
where the time goes in v1:
time: 114 us
  waiting for transfers between devices  47.6 us (42%)
  blocking collectives  42.2 us (37%)
  Pallas kernels  10.5 us (9%)
  starting transfers between devices  7.45 us (7%)
  local copies, waits for them, and re-layouts  4.58 us (4%)
    all_to_all x1, waiting for transfers between devices, lines(): moved = lax.all_to_all(moved, ('chan', 'range'), 0, 0, tiled=True)  47.6 us
    all_to_all x1, blocking collectives, lines(): columns = lax.all_to_all(compressed, everyone, 0, 0, tiled=True)  30.9 us
    all_to_all x1, blocking collectives, lines(): found = lax.all_to_all(found, ('pulse', 'range'), 0, 0, tiled=True)  11.2 us
    pallas_call x2, Pallas kernels, vmem_call(): pl.pallas_call(kernel, out_shape=out_shape, in_specs=[pl.BlockSpec(memory...  10.5 us
    all_to_all x1, starting transfers between devices, lines(): moved = lax.all_to_all(moved, ('chan', 'range'), 0, 0, tiled=True)  7.45 us
    unnamed x17, local copies, waits for them, and re-layouts  4.12 us
  transfers between devices with their start and end apart: 1, of which 1 were waited for; matrix products, arithmetic and copies ran while one was open for 0% of the time, Pallas kernels for 0%

profile of v1, /device:TPU:0, one launch (start us, length us, event | category | flops | bytes accessed | tf_op | source)
XLA Modules:
  0.0 113.6 jit_solution(15639073427115851939)
XLA Ops:
  0.0 4.1 %copy.25 = bf16[2,16,8,4096]{3,1,0,2:T(8,128)(2,1)} copy(bf16[2,16,8,4096]{3,2,1,0:T(8,128)(2,1)} %param.9) | data formatting | bytes 4194304 | tf_op args[0]
  4.1 0.0 copy-start.2
  4.1 0.0 copy-start.3
  4.1 0.0 copy-start.4
  4.1 7.5 %all-to-all-start = ((bf16[8,2,16,4096]{3,2,1,0:T(8,128)(2,1)}), bf16[8,2,16,4096]{3,2,1,0:T(8,128)(2,1)S(1)}, u32[]{:S(2)}, u32[]{:S(2)}) async-start(bf16[8,2,16,4096]{3,2,1,0:T(8,128)(2,1)} %bitcast.19), calls=%async_computation | async-start | bytes 4194304 | tf_op jit(solution)/shard_map/all_to_all | solution.py:163
  11.6 0.0 copy-done.7
  11.6 0.1 maximum_maximum_fusion
  11.7 0.1 copy.19
  11.9 0.1 copy.22.w_ref
  12.0 0.0 copy-done.6
  12.0 0.1 reshape.27
  12.1 0.1 copy.21
  12.2 47.6 %all-to-all-done = bf16[8,2,16,4096]{3,2,1,0:T(8,128)(2,1)S(1)} async-done(((bf16[8,2,16,4096]{3,2,1,0:T(8,128)(2,1)}), bf16[8,2,16,4096]{3,2,1,0:T(8,128)(2,1)S(1)}, u32[]{:S(2)}, u32[]{:S(2)}) %all-to-all-start) | async-done | bytes 2097184 | tf_op jit(solution)/shard_map/all_to_all | solution.py:163
  59.8 0.0 copy-done
  59.8 0.0 copy-done.1
  59.8 0.0 copy-done.2
  59.8 0.0 copy-done.3
  59.8 0.0 copy-done.4
  59.8 6.4 %shard_map.91 = bf16[32,128,128]{2,1,0:T(8,128)(2,1)S(1)} custom-call(bf16[4,2,2,16,4096]{4,3,2,1,0:T(8,128)(2,1)S(1)} %bitcast.16, bf16[64,128]{1,0:T(8,128)(2,1)S(1)} %copy.22.w_ref, bf16[128,128]{1,0:T(8,128)(2,1)S(1)} %copy-done.3, bf16[128,128]{1,0:T(8,128)(2,1)S(1)} %copy-done.4, bf16[256,256]{1,0:T(8,128)(2,1)S(1)} %copy-done, ...), custom_call_target="tpu_custom_call" | custom-call | flops 2000000000 | tf_op jit(solution)/shard_map/pallas_call | solution.py:141
  66.2 0.0 copy-start.5
  66.2 30.9 %all_to_all.15.z_ref = bf16[32,128,128]{2,1,0:T(8,128)(2,1)S(1)} all-to-all(bf16[32,128,128]{2,1,0:T(8,128)(2,1)S(1)} %shard_map.91), channel_id=1, replica_groups=mesh['chan'=4,'pulse'=4,'range'=2] {'pulse','chan','range'}, dimensions={0} | all-to-all | bytes 2097152 | tf_op jit(solution)/shard_map/all_to_all | solution.py:182
  97.2 4.1 %shard_map.92 = bf16[4,2,8,4096]{3,2,1,0:T(8,128)(2,1)S(1)} custom-call(bf16[32,128,128]{2,1,0:T(8,128)(2,1)S(1)} %all_to_all.15.z_ref, bf16[64,64]{1,0:T(8,128)(2,1)S(1)} %copy-done.5), custom_call_target="tpu_custom_call" | custom-call | flops 2000000000 | tf_op jit(solution)/shard_map/pallas_call | solution.py:141
  101.3 11.2 %all_to_all.16 = bf16[8,8,4096]{2,1,0:T(8,128)(2,1)S(1)} all-to-all(bf16[8,8,4096]{2,1,0:T(8,128)(2,1)S(1)} %bitcast.17), channel_id=1, replica_groups=mesh['chan'=4,'pulse'=4,'range'=2] {'pulse','range'}, dimensions={0} | all-to-all | bytes 1048576 | tf_op jit(solution)/shard_map/all_to_all | solution.py:195
  112.5 1.0 convert_element_type.3
  (9 shorter events, 0.0 us)
Async XLA Ops:
  4.1 7.5 %copy-start.7 = (bf16[2,32,64]{2,1,0:T(8,128)(2,1)S(1)}, bf16[2,32,64]{2,1,0:T(8,128)(2,1)}, u32[]{:S(2)}) copy-start(bf16[2,32,64]{2,1,0:T(8,128)(2,1)} %param.10) | copy-start | bytes 24580
  4.1 7.9 %copy-start.6 = (f32[2,8192]{1,0:T(2,128)S(1)}, f32[2,8192]{1,0:T(2,128)}, u32[]{:S(2)}) copy-start(f32[2,8192]{1,0:T(2,128)} %param.11) | copy-start | bytes 196612
  4.1 55.7 %copy-start = (bf16[256,256]{1,0:T(8,128)(2,1)S(1)}, bf16[256,256]{1,0:T(8,128)(2,1)}, u32[]{:S(2)}) copy-start(bf16[256,256]{1,0:T(8,128)(2,1)} %constant.14.clone.rf_ref) | copy-start | bytes 393220
  4.1 55.7 %copy-start.1 = (bf16[256,256]{1,0:T(8,128)(2,1)S(1)}, bf16[256,256]{1,0:T(8,128)(2,1)}, u32[]{:S(2)}) copy-start(bf16[256,256]{1,0:T(8,128)(2,1)} %constant.15.clone.ri_ref) | copy-start | bytes 393220
  4.1 55.7 %copy-start.2 = (f32[2,64,128]{2,1,0:T(8,128)S(1)}, f32[2,64,128]{2,1,0:T(8,128)}, u32[]{:S(2)}) copy-start(f32[2,64,128]{2,1,0:T(8,128)} %constant.16.clone.tw_ref) | copy-start | bytes 196612
  4.1 55.7 %copy-start.3 = (bf16[128,128]{1,0:T(8,128)(2,1)S(1)}, bf16[128,128]{1,0:T(8,128)(2,1)}, u32[]{:S(2)}) copy-start(bf16[128,128]{1,0:T(8,128)(2,1)} %constant.12.clone.lf_ref) | copy-start | bytes 98308
  4.1 55.7 %copy-start.4 = (bf16[128,128]{1,0:T(8,128)(2,1)S(1)}, bf16[128,128]{1,0:T(8,128)(2,1)}, u32[]{:S(2)}) copy-start(bf16[128,128]{1,0:T(8,128)(2,1)} %constant.13.clone.li_ref) | copy-start | bytes 98308
  4.1 55.7 %all-to-all-start = ((bf16[8,2,16,4096]{3,2,1,0:T(8,128)(2,1)}), bf16[8,2,16,4096]{3,2,1,0:T(8,128)(2,1)S(1)}, u32[]{:S(2)}, u32[]{:S(2)}) async-start(bf16[8,2,16,4096]{3,2,1,0:T(8,128)(2,1)} %bitcast.19), calls=%async_computation | async-start | bytes 4194304 | tf_op jit(solution)/shard_map/all_to_all | solution.py:163
  66.2 31.0 %copy-start.5 = (bf16[64,64]{1,0:T(8,128)(2,1)S(1)}, bf16[64,64]{1,0:T(8,128)(2,1)}, u32[]{:S(2)}) copy-start(bf16[64,64]{1,0:T(8,128)(2,1)} %constant.17.clone.d_ref) | copy-start | bytes 24580
